TPU v7x, 512 devices: a whole 4x8x8 slice. The times are simulated.
512 devices in a mesh: dom: 32 (over z, x), snap: 16 (over y, core).
Axes of the slice: x: 4, y: 8, z: 8, core: 2. Of those that a mesh axis runs over, the one named last changes fastest.
Arguments:
- feat: bfloat16 [16, 4096, 512], P('snap', 'dom'), may hold values from -6 to 6
- w_struct: bfloat16 [512, 1536], replicated, may hold values from -0.25 to 0.25
- w_temp: bfloat16 [512, 1536], replicated, may hold values from -0.25 to 0.25
- pos_embed: bfloat16 [16, 512], replicated, may hold values from -3 to 3
- rel_bias: float32 [4, 8], replicated, may hold values from -1.5 to 1.5
- nbr: int32 [16, 4096, 8], P('snap', 'dom'), may hold values from 0 to 383
- rel_type: int32 [16, 4096, 8], P('snap', 'dom'), may hold values from 0 to 3
- send_idx: int32 [16, 32, 32, 8], P('snap', 'dom'), may hold values from 0 to 127
- active: int32 [16, 4096], P(None, ('dom', 'snap')), may hold values 0 or 1
- cotangent: bfloat16 [16, 4096, 512], P(None, ('dom', 'snap')), may hold values from -6 to 6
Outputs:
- grad_feat: bfloat16 [16, 4096, 512], P('snap', 'dom')
- grad_wtemp: float32 [512, 1536], P('snap')
Inputs may be any that keep to these rules, and one draw needn't show every extreme that they name: `nbr`: rows of the partition's key table: its 128 own entities first, then 8 halo rows from each partition in order.
All inputs are finite; a program needn't handle non-finite values. No bound on the sum of `active` on one device may be relied on, other than what follows from the above.
Results may differ from a plain program's by a relative error of at most 0.024.
Values may be sent and summed in bfloat16 or wider, within the bound.
A program may use at most 64 MiB of HBM per device.

v0:
```python
import jax
import jax.numpy as jnp
from jax import lax
from jax.sharding import PartitionSpec as P

HEADS = 8


def edge_scores(rel_ids, rel_bias):
    onehot = (rel_ids[..., None] == jnp.arange(rel_bias.shape[0], dtype=jnp.int32)).astype(
        jnp.float32
    )
    return jnp.einsum("rek,kh->reh", onehot, rel_bias, precision=lax.Precision.HIGHEST)


def struct_core(query, key_tab, val_tab, links, edge_add):
    row_count, width = query.shape
    slots = links.shape[1]
    head_dim = width // HEADS
    keys_g = key_tab[links].reshape(row_count, slots, HEADS, head_dim)
    vals_g = val_tab[links].reshape(row_count, slots, HEADS, head_dim)
    query_h = query.reshape(row_count, HEADS, head_dim)
    scores = jnp.einsum("rhc,rehc->reh", query_h, keys_g) * head_dim ** (-0.5) + edge_add
    weights = jax.nn.softmax(scores, axis=1)
    rounded = lax.optimization_barrier(weights.astype(jnp.bfloat16)).astype(jnp.float32)
    return jnp.einsum("reh,rehc->rhc", rounded, vals_g).reshape(row_count, width)


def temp_allowed(active_blk):
    snaps = active_blk.shape[0]
    later = jnp.arange(snaps, dtype=jnp.int32)[:, None]
    earlier = jnp.arange(snaps, dtype=jnp.int32)[None, :]
    causal = (earlier <= later)[..., None]
    itself = (earlier == later)[..., None]
    return causal & (itself | (active_blk[None, :, :] == 1))


def temp_core(t_query, t_key, t_value, allowed):
    snaps, count, width = t_query.shape
    head_dim = width // HEADS
    query_h = t_query.reshape(snaps, count, HEADS, head_dim)
    key_h = t_key.reshape(snaps, count, HEADS, head_dim)
    value_h = t_value.reshape(snaps, count, HEADS, head_dim)
    scores = jnp.einsum("tmhc,umhc->tumh", query_h, key_h) * head_dim ** (-0.5)
    scores = jnp.where(allowed[..., None], scores, -1e30)
    weights = jax.nn.softmax(scores, axis=1)
    rounded = lax.optimization_barrier(weights.astype(jnp.bfloat16)).astype(jnp.float32)
    return jnp.einsum("tumh,umhc->tmhc", rounded, value_h).reshape(snaps, count, width)


def per_device(
    feat, w_struct, w_temp, pos_embed, rel_bias, nbr, rel_type, send_idx, active, cotangent
):
    x_rows = feat[0]
    local_count, width = x_rows.shape
    dom_count = lax.axis_size("dom")
    route = send_idx[0, 0]
    halo_per = route.shape[1]
    route_flat = route.reshape(-1)
    projected = jnp.dot(x_rows, w_struct, preferred_element_type=jnp.float32).astype(jnp.bfloat16)
    pair_cols = projected[:, width:]
    tiles = pair_cols[route_flat].reshape(dom_count, halo_per, 2 * width)
    arrived = lax.all_to_all(tiles, "dom", split_axis=0, concat_axis=0, tiled=True).reshape(
        -1, 2 * width
    )
    query_f = projected[:, :width].astype(jnp.float32)
    table = jnp.concatenate([pair_cols, arrived], axis=0).astype(jnp.float32)
    edge_add = edge_scores(rel_type[0], rel_bias)
    links = nbr[0]
    summed = struct_core(query_f, table[:, :width], table[:, width:], links, edge_add)
    hidden = (x_rows.astype(jnp.float32) + jax.nn.elu(summed)).astype(jnp.bfloat16)
    by_entity = lax.all_to_all(hidden[None], "snap", split_axis=1, concat_axis=0, tiled=True)
    snaps = by_entity.shape[0]
    z_in = (by_entity.astype(jnp.float32) + pos_embed.astype(jnp.float32)[:, None, :]).astype(
        jnp.bfloat16
    )
    z_flat = z_in.reshape(-1, width)
    t_proj = jnp.dot(z_flat, w_temp, preferred_element_type=jnp.float32).astype(jnp.bfloat16)
    t_proj = t_proj.reshape(snaps, -1, 3 * width).astype(jnp.float32)
    allowed = temp_allowed(active)
    cot_f = cotangent.astype(jnp.float32)
    _, pull = jax.vjp(
        lambda a_in, b_in, c_in: temp_core(a_in, b_in, c_in, allowed),
        t_proj[..., :width],
        t_proj[..., width : 2 * width],
        t_proj[..., 2 * width :],
    )
    grads_t = pull(cot_f)
    dt_proj = jnp.concatenate(grads_t, axis=-1).astype(jnp.bfloat16).reshape(-1, 3 * width)
    terms = lax.dot_general(
        z_flat, dt_proj, (((0,), (0,)), ((), ())), preferred_element_type=jnp.float32
    )
    share = lax.psum_scatter(terms.astype(jnp.bfloat16), "snap", scatter_dimension=0, tiled=True)
    grad_wtemp = lax.psum(share, "dom").astype(jnp.float32)
    d_z = cot_f + jnp.dot(dt_proj, w_temp.T, preferred_element_type=jnp.float32).reshape(
        snaps, -1, width
    )
    returned = lax.all_to_all(
        d_z.astype(jnp.bfloat16), "snap", split_axis=0, concat_axis=1, tiled=True
    )[0]
    dh_f = returned.astype(jnp.float32)
    d_agg = dh_f * jnp.where(summed > 0, 1.0, jnp.exp(summed))
    _, pull_s = jax.vjp(
        lambda a_in, b_in, c_in: struct_core(a_in, b_in, c_in, links, edge_add),
        query_f,
        table[:, :width],
        table[:, width:],
    )
    d_query, d_key, d_val = pull_s(d_agg)
    halo_back = jnp.concatenate([d_key[local_count:], d_val[local_count:]], axis=-1)
    halo_back = halo_back.reshape(dom_count, halo_per, 2 * width)
    came_back = (
        lax.all_to_all(
            halo_back.astype(jnp.bfloat16), "dom", split_axis=0, concat_axis=0, tiled=True
        )
        .astype(halo_back.dtype)
        .reshape(-1, 2 * width)
    )
    owned = jnp.concatenate([d_key[:local_count], d_val[:local_count]], axis=-1)
    owned = owned.at[route_flat].add(came_back)
    d_proj = jnp.concatenate([d_query, owned], axis=-1).astype(jnp.bfloat16)
    grad_rows = (dh_f + jnp.dot(d_proj, w_struct.T, preferred_element_type=jnp.float32)).astype(
        jnp.bfloat16
    )
    return (grad_rows[None], grad_wtemp)


def solution(mesh):
    return jax.shard_map(
        per_device,
        mesh=mesh,
        in_specs=(
            P("snap", "dom", None),
            P(),
            P(),
            P(),
            P(),
            P("snap", "dom", None),
            P("snap", "dom", None),
            P("snap", "dom", None, None),
            P(None, ("dom", "snap")),
            P(None, ("dom", "snap"), None),
        ),
        out_specs=(P("snap", "dom", None), P("snap", None)),
        check_vma=False,
    )
```

profile of v0, /device:TPU:8, one launch (start us, length us, event | category | flops | bytes accessed | tf_op | source)
XLA Modules:
  0.0 353.8 jit_solution(8830739789273474780)
XLA Ops:
  8.2 1.9 convolution_convert_fusion.1
  10.3 2.0 gather_fusion
  12.3 13.3 %all-to-all-start = ((bf16[32,8,1024]{2,1,0:T(8,128)(2,1)}), bf16[32,8,1024]{2,1,0:T(8,128)(2,1)S(1)}, u32[]{:S(2)}, u32[]{:S(2)}) async-start(bf16[32,8,1024]{2,1,0:T(8,128)(2,1)} %bitcast.7), calls=%async_computation | async-start | bytes 1048576 | tf_op jit(solution)/shard_map/all_to_all | solution.py:63
  27.3 16.1 %all-to-all-done = bf16[32,8,1024]{2,1,0:T(8,128)(2,1)S(1)} async-done(((bf16[32,8,1024]{2,1,0:T(8,128)(2,1)}), bf16[32,8,1024]{2,1,0:T(8,128)(2,1)S(1)}, u32[]{:S(2)}, u32[]{:S(2)}) %all-to-all-start) | async-done | bytes 524320 | tf_op jit(solution)/shard_map/all_to_all | solution.py:63
  45.2 5.1 %gather_fusion.1 = bf16[1024,512]{1,0:T(8,128)(2,1)} fusion(bf16[384,512]{1,0:T(8,128)(2,1)S(1)} %get-tuple-element.3, s32[1024]{0:T(1024)S(1)} %get-tuple-element.20), kind=kCustom, calls=%fused_computation.1 | custom fusion | bytes 2101248 | tf_op jit(solution)/shard_map/gather | solution.py:20
  50.3 3.9 %reshape.244 = bf16[128,8,8,64]{3,2,1,0:T(8,128)(2,1)} reshape(bf16[1024,512]{1,0:T(8,128)(2,1)} %gather_fusion.1) | data formatting | bytes 2097152 | tf_op jit(solution)/shard_map/reshape | solution.py:20
  54.2 3.6 %multiply_reduce_fusion.3 = f32[128,8,8]{1,2,0:T(8,128)} fusion(f32[128,8,64]{2,1,0:T(8,128)S(1)} %copy.120, bf16[128,8,8,64]{3,2,1,0:T(8,128)(2,1)} %reshape.244), kind=kLoop, calls=%fused_computation.10 | loop fusion | flops 1564672 | bytes 1343488
  60.3 5.1 %gather_fusion.2 = bf16[1024,512]{1,0:T(8,128)(2,1)} fusion(bf16[384,512]{1,0:T(8,128)(2,1)S(1)} %get-tuple-element.2, s32[1024]{0:T(1024)S(1)} %get-tuple-element.20), kind=kCustom, calls=%fused_computation.2 | custom fusion | bytes 2101248 | tf_op jit(solution)/shard_map/gather | solution.py:21
  65.4 4.0 %reshape.246 = bf16[128,8,8,64]{3,2,1,0:T(8,128)(2,1)} reshape(bf16[1024,512]{1,0:T(8,128)(2,1)} %gather_fusion.2) | data formatting | bytes 2097152 | tf_op jit(solution)/shard_map/reshape | solution.py:21
  69.3 2.6 multiply_reduce_fusion.2
  76.1 7.6 %all-to-all-start.1 = ((bf16[16,2,2048]{2,1,0:T(2,128)(2,1)}), bf16[16,2,2048]{2,1,0:T(2,128)(2,1)S(1)}, u32[]{:S(2)}, u32[]{:S(2)}) async-start(bf16[16,2,2048]{2,1,0:T(2,128)(2,1)} %reshape.337), calls=%async_computation.1 | async-start | bytes 262144 | tf_op jit(solution)/shard_map/all_to_all | solution.py:72
  84.2 6.8 %all-to-all-done.1 = bf16[16,2,2048]{2,1,0:T(2,128)(2,1)S(1)} async-done(((bf16[16,2,2048]{2,1,0:T(2,128)(2,1)}), bf16[16,2,2048]{2,1,0:T(2,128)(2,1)S(1)}, u32[]{:S(2)}, u32[]{:S(2)}) %all-to-all-start.1) | async-done | bytes 131104 | tf_op jit(solution)/shard_map/all_to_all | solution.py:72
  98.0 2.1 fusion.76
  100.9 2.3 fusion.10
  103.2 2.2 fusion.11
  113.7 2.9 fusion.1
  117.9 4.7 %all-to-all-start.2 = ((bf16[16,8,512]{2,1,0:T(8,128)(2,1)}), bf16[16,8,512]{2,1,0:T(8,128)(2,1)S(1)}, u32[]{:S(2)}, u32[]{:S(2)}) async-start(bf16[16,8,512]{2,1,0:T(8,128)(2,1)} %fusion.17), calls=%async_computation.2 | async-start | bytes 262144 | tf_op jit(solution)/shard_map/all_to_all | solution.py:98
  123.6 6.6 %all-to-all-done.2 = bf16[16,8,512]{2,1,0:T(8,128)(2,1)S(1)} async-done(((bf16[16,8,512]{2,1,0:T(8,128)(2,1)}), bf16[16,8,512]{2,1,0:T(8,128)(2,1)S(1)}, u32[]{:S(2)}, u32[]{:S(2)}) %all-to-all-start.2) | async-done | bytes 131104 | tf_op jit(solution)/shard_map/all_to_all | solution.py:98
  130.9 5.6 %multiply_reduce_fusion.1 = (bf16[128,8,8]{1,2,0:T(8,128)(2,1)S(1)}, f32[128,8,8,64]{3,2,1,0:T(8,128)}) fusion(f32[128,8,64]{2,1,0:T(8,128)S(1)} %copy.122, bf16[128,8,8,64]{3,2,1,0:T(8,128)(2,1)} %reshape.246, f32[128,8,8]{1,2,0:T(8,128)} %copy.90), kind=kLoop, calls=%fused_computation.8 | loop fusion | flops 2088960 | bytes 3457024
  136.5 4.8 %reshape.300 = f32[1024,512]{1,0:T(8,128)} reshape(f32[128,8,8,64]{3,2,1,0:T(8,128)} %get-tuple-element.7) | data formatting | bytes 4194304 | tf_op jit(solution)/shard_map/transpose(jvp())/reshape | solution.py:21
  141.7 5.6 %multiply_reduce_fusion = (bf16[128,8,64]{2,1,0:T(8,128)(2,1)}, f32[128,8,8,64]{3,2,1,0:T(8,128)}) fusion(f32[128,8,8]{1,2,0:T(8,128)S(1)} %copy.123, bf16[128,8,8,64]{3,2,1,0:T(8,128)(2,1)} %reshape.244, f32[128,8,64]{2,1,0:T(8,128)S(1)} %copy.120), kind=kLoop, calls=%fused_computation.7 | loop fusion | flops 2031616 | bytes 3571712
  147.4 4.8 %reshape.292 = f32[1024,512]{1,0:T(8,128)} reshape(f32[128,8,8,64]{3,2,1,0:T(8,128)} %get-tuple-element.5) | data formatting | bytes 4194304 | tf_op jit(solution)/shard_map/transpose(jvp())/reshape | solution.py:20
  152.2 7.5 %scatter_custom_fusion.1 = f32[384,512]{1,0:T(8,128)S(1)} fusion(s32[1024]{0:T(1024)S(1)} %reshape.274, f32[1024,512]{1,0:T(8,128)} %reshape.300, f32[]{:T(128)} %constant.15.clone.1), kind=kCustom, calls=%fused_computation.65 | custom fusion | flops 524288 | bytes 786944 | tf_op jit(solution)/shard_map/transpose(jvp())/scatter-add | solution.py:21
  159.7 7.5 %scatter_custom_fusion = f32[384,512]{1,0:T(8,128)S(1)} fusion(s32[1024]{0:T(1024)S(1)} %reshape.274, f32[1024,512]{1,0:T(8,128)} %reshape.292, f32[]{:T(128)} %constant.15.clone.1), kind=kCustom, calls=%fused_computation.67 | custom fusion | flops 524288 | bytes 786944 | tf_op jit(solution)/shard_map/transpose(jvp())/scatter-add | solution.py:20
  168.2 4.6 %all-to-all-start.3 = ((bf16[32,8,1024]{2,1,0:T(8,128)(2,1)}), bf16[32,8,1024]{2,1,0:T(8,128)(2,1)}, u32[]{:S(2)}, u32[]{:S(2)}) async-start(bf16[32,8,1024]{2,1,0:T(8,128)(2,1)} %maximum_bitcast_fusion), calls=%async_computation.3 | async-start | bytes 1048576 | tf_op jit(solution)/shard_map/all_to_all | solution.py:113
  173.2 1.8 slice.61
  175.0 1.8 copy.119
  178.4 1.8 pad_maximum_fusion
  180.2 10.9 %all-to-all-done.3 = bf16[32,8,1024]{2,1,0:T(8,128)(2,1)} async-done(((bf16[32,8,1024]{2,1,0:T(8,128)(2,1)}), bf16[32,8,1024]{2,1,0:T(8,128)(2,1)}, u32[]{:S(2)}, u32[]{:S(2)}) %all-to-all-start.3) | async-done | bytes 524320 | tf_op jit(solution)/shard_map/all_to_all | solution.py:113
  191.1 5.0 %scatter_custom_fusion.2 = f32[128,1024]{1,0:T(8,128)} fusion(f32[128,1024]{1,0:T(8,128)} %pad_maximum_fusion, s32[256]{0:T(256)S(1)} %bitcast.139, bf16[32,8,1024]{2,1,0:T(8,128)(2,1)} %all-to-all-done.3), kind=kCustom, calls=%fused_computation.39 | custom fusion | flops 524288 | bytes 1048576 | tf_op jit(solution)/shard_map/scatter-add | solution.py:120
  197.3 2.2 fusion.20
  199.5 145.9 %all-reduce.2.cloned.1.call-done = bf16[32,1536]{1,0:T(8,128)(2,1)} async-done(((bf16[32,1536]{1,0:T(8,128)(2,1)}), bf16[32,1536]{1,0:T(8,128)(2,1)}) %all-reduce.2.cloned.1.call-update) | async-done | bytes 98320 | tf_op jit(solution)/shard_map/psum | solution.py:94
  (116 shorter events, 37.0 us)
Async XLA Ops:
  7.2 84.0 %copy-start = (bf16[512,1536]{1,0:T(8,128)(2,1)S(1)}, bf16[512,1536]{1,0:T(8,128)(2,1)}, u32[]{:S(2)}) copy-start(bf16[512,1536]{1,0:T(8,128)(2,1)} %param.12) | copy-start | bytes 4718596
  7.2 2.9 copy-start.15
  10.3 15.3 %copy-start.12 = (bf16[1,128,512]{2,1,0:T(8,128)(2,1)S(1)}, bf16[1,128,512]{2,1,0:T(8,128)(2,1)}, u32[]{:S(2)}) copy-start(bf16[1,128,512]{2,1,0:T(8,128)(2,1)} %param.10) | copy-start | bytes 393220
  12.3 14.4 %copy-start.17 = (s32[16,8]{0,1:T(8,128)S(1)}, s32[16,8]{0,1:T(8,128)}, u32[]{:S(2)}) copy-start(s32[16,8]{0,1:T(8,128)} %param.18) | copy-start | bytes 1540
  12.3 31.1 %all-to-all-start = ((bf16[32,8,1024]{2,1,0:T(8,128)(2,1)}), bf16[32,8,1024]{2,1,0:T(8,128)(2,1)S(1)}, u32[]{:S(2)}, u32[]{:S(2)}) async-start(bf16[32,8,1024]{2,1,0:T(8,128)(2,1)} %bitcast.7), calls=%async_computation | async-start | bytes 1048576 | tf_op jit(solution)/shard_map/all_to_all | solution.py:63
  43.3 0.8 copy-start.3
  54.2 4.8 %copy-start.16 = (s32[1,128,8]{1,2,0:T(8,128)S(1)}, s32[1,128,8]{1,2,0:T(8,128)}, u32[]{:S(2)}) copy-start(s32[1,128,8]{1,2,0:T(8,128)} %param.16) | copy-start | bytes 12292
  54.2 4.8 %copy-start.19 = (f32[4,8]{1,0:T(4,128)S(1)}, f32[4,8]{1,0:T(4,128)}, u32[]{:S(2)}) copy-start(f32[4,8]{1,0:T(4,128)} %param.14) | copy-start | bytes 388
  65.4 4.0 %copy-start.4 = (f32[128,8,8]{1,2,0:T(8,128)S(1)}, f32[128,8,8]{1,2,0:T(8,128)}, u32[]{:S(2)}) copy-start(f32[128,8,8]{1,2,0:T(8,128)} %copy.121) | copy-start | bytes 98308
  71.9 11.9 %copy-start.14 = (bf16[16,512]{1,0:T(8,128)(2,1)S(1)}, bf16[16,512]{1,0:T(8,128)(2,1)}, u32[]{:S(2)}) copy-start(bf16[16,512]{1,0:T(8,128)(2,1)} %param.13) | copy-start | bytes 49156
  71.9 11.9 %copy-start.10 = (bf16[16,8,512]{2,1,0:T(8,128)(2,1)S(1)}, bf16[16,8,512]{2,1,0:T(8,128)(2,1)}, u32[]{:S(2)}) copy-start(bf16[16,8,512]{2,1,0:T(8,128)(2,1)} %param.19) | copy-start | bytes 393220
  71.9 12.1 %copy-start.18 = (pred[16,8]{0,1:T(8,128)(4,1)S(1)}, pred[16,8]{0,1:T(8,128)(4,1)}, u32[]{:S(2)}) copy-start(pred[16,8]{0,1:T(8,128)(4,1)} %broadcast_compare_fusion) | copy-start | bytes 388
  76.1 14.9 %all-to-all-start.1 = ((bf16[16,2,2048]{2,1,0:T(2,128)(2,1)}), bf16[16,2,2048]{2,1,0:T(2,128)(2,1)S(1)}, u32[]{:S(2)}, u32[]{:S(2)}) async-start(bf16[16,2,2048]{2,1,0:T(2,128)(2,1)} %reshape.337), calls=%async_computation.1 | async-start | bytes 262144 | tf_op jit(solution)/shard_map/all_to_all | solution.py:72
  83.6 113.6 %reduce-scatter.2.cloned.1.call-start = ((), (), s32[]{:S(2)}) async-start(), calls=%async_computation.5 | async-start | bytes 1671168 | tf_op jit(solution)/shard_map/reduce_scatter | solution.py:93
  84.2 12.4 %copy-start.13 = (pred[16,16,8]{0,1,2:T(8,128)(4,1)}, pred[16,16,8]{0,1,2:T(8,128)(4,1)S(1)}, u32[]{:S(2)}) copy-start(pred[16,16,8]{0,1,2:T(8,128)(4,1)S(1)} %or_and_fusion) | copy-start | bytes 6148
  91.1 1.1 copy-start.8
  93.4 6.7 %copy-start.6 = (bf16[16,8,8,64]{3,2,1,0:T(8,128)(2,1)}, bf16[16,8,8,64]{3,2,1,0:T(8,128)(2,1)S(1)}, u32[]{:S(2)}) copy-start(bf16[16,8,8,64]{3,2,1,0:T(8,128)(2,1)S(1)} %reshape.251) | copy-start | bytes 393220
  96.6 3.5 copy-start.5
  105.4 8.2 %copy-start.9 = (bf16[128,1,512]{2,1,0:T(2,128)(2,1)S(1)}, bf16[128,1,512]{2,1,0:T(2,128)(2,1)}, u32[]{:S(2)}) copy-start(bf16[128,1,512]{2,1,0:T(2,128)(2,1)} %copy-done.8) | copy-start | bytes 393220
  113.7 2.9 copy-start.7
  113.7 3.0 copy-start.11
  117.9 12.2 %all-to-all-start.2 = ((bf16[16,8,512]{2,1,0:T(8,128)(2,1)}), bf16[16,8,512]{2,1,0:T(8,128)(2,1)S(1)}, u32[]{:S(2)}, u32[]{:S(2)}) async-start(bf16[16,8,512]{2,1,0:T(8,128)(2,1)} %fusion.17), calls=%async_computation.2 | async-start | bytes 262144 | tf_op jit(solution)/shard_map/all_to_all | solution.py:98
  167.1 6.0 %copy-start.2 = (f32[384,512]{1,0:T(8,128)}, f32[384,512]{1,0:T(8,128)S(1)}, u32[]{:S(2)}) copy-start(f32[384,512]{1,0:T(8,128)S(1)} %scatter_custom_fusion) | copy-start | bytes 2359300
  168.2 22.9 %all-to-all-start.3 = ((bf16[32,8,1024]{2,1,0:T(8,128)(2,1)}), bf16[32,8,1024]{2,1,0:T(8,128)(2,1)}, u32[]{:S(2)}, u32[]{:S(2)}) async-start(bf16[32,8,1024]{2,1,0:T(8,128)(2,1)} %maximum_bitcast_fusion), calls=%async_computation.3 | async-start | bytes 1048576 | tf_op jit(solution)/shard_map/all_to_all | solution.py:113
  172.8 172.5 %all-reduce.2.cloned.1.call-start = ((), (), s32[]{:S(2)}) async-start(), calls=%async_computation.6 | async-start | bytes 196608 | tf_op jit(solution)/shard_map/psum | solution.py:94
  173.2 24.1 %copy-start.1 = (bf16[512,1536]{1,0:T(8,128)(2,1)S(1)}, bf16[512,1536]{1,0:T(8,128)(2,1)}, u32[]{:S(2)}) copy-start(bf16[512,1536]{1,0:T(8,128)(2,1)} %param.11) | copy-start | bytes 4718596
Sparse Core Ops, SparseCore 0:
  116.7 52.3 reduce-scatter.1
  197.4 147.9 all-reduce.1
where the time goes:
time: 355 us; the launch traced here: 354 us
  waiting for transfers between devices  186 us (52%)
  local copies, waits for them, and re-layouts  55.2 us (16%)
  other arithmetic  50.8 us (14%)
  starting transfers between devices  30.7 us (9%)
  matrix products  16.1 us (5%)
  between operations  14.6 us (4%)
    psum x1, waiting for transfers between devices, per_device(): grad_wtemp = lax.psum(share, 'dom').astype(jnp.float32)  146 us
    unnamed x5, other arithmetic  18.8 us
    all_to_all x1, waiting for transfers between devices, per_device(): lax.all_to_all(tiles, 'dom', split_axis=0, concat_axis=0, tiled=True)  16.1 us
    all_to_all x1, starting transfers between devices, per_device(): lax.all_to_all(tiles, 'dom', split_axis=0, concat_axis=0, tiled=True)  13.3 us
    all_to_all x1, waiting for transfers between devices, per_device(): lax.all_to_all(halo_back.astype(jnp.bfloat16), 'dom', split_axis=0, conca...  10.9 us
    reshape x2, local copies, waits for them, and re-layouts, struct_core(): vals_g = val_tab[links].reshape(row_count, slots, HEADS, head_dim)  8.76 us
    reshape x2, local copies, waits for them, and re-layouts, struct_core(): keys_g = key_tab[links].reshape(row_count, slots, HEADS, head_dim)  8.71 us
    unnamed x51, local copies, waits for them, and re-layouts  7.9 us
  transfers between devices with their start and end apart: 6, of which 5 were waited for; matrix products, arithmetic and copies ran while one was open for 16% of the time, Pallas kernels for 0%

commit v1 on v0

--- a/solution.py
+++ b/solution.py
@@ -4,6 +4,11 @@
 from jax.sharding import PartitionSpec as P
 
 HEADS = 8
+
+
+def gather_and_add(value, axis):
+    parts = lax.all_gather(value, axis)
+    return jnp.sum(parts, axis=0)
 
 
 def edge_scores(rel_ids, rel_bias):
@@ -91,7 +96,7 @@
         z_flat, dt_proj, (((0,), (0,)), ((), ())), preferred_element_type=jnp.float32
     )
     share = lax.psum_scatter(terms.astype(jnp.bfloat16), "snap", scatter_dimension=0, tiled=True)
-    grad_wtemp = lax.psum(share, "dom").astype(jnp.float32)
+    grad_wtemp = gather_and_add(share, "dom").astype(jnp.float32)
     d_z = cot_f + jnp.dot(dt_proj, w_temp.T, preferred_element_type=jnp.float32).reshape(
         snaps, -1, width
     )

time: 355 us -> 278 us (0.78)
  the two profiles are of different devices: /device:TPU:8 before, /device:TPU:1 now
where the time goes in v1:
time: 278 us; the launch traced here: 277 us
  waiting for transfers between devices  97.5 us (35%)
  local copies, waits for them, and re-layouts  55.4 us (20%)
  other arithmetic  52.2 us (19%)
  starting transfers between devices  40.7 us (15%)
  matrix products  16.1 us (6%)
  between operations  14.6 us (5%)
    reduce_scatter x1, waiting for transfers between devices, per_device(): lax.psum_scatter(terms.astype(jnp.bfloat16), 'snap', scatter_dimension=0,...  51 us
    unnamed x5, other arithmetic  18.8 us
    all_to_all x1, waiting for transfers between devices, per_device(): lax.all_to_all(halo_back.astype(jnp.bfloat16), 'dom', split_axis=0, conca...  15.7 us
    all_to_all x1, waiting for transfers between devices, per_device(): lax.all_to_all(tiles, 'dom', split_axis=0, concat_axis=0, tiled=True)  14.6 us
    all_to_all x1, starting transfers between devices, per_device(): lax.all_to_all(tiles, 'dom', split_axis=0, concat_axis=0, tiled=True)  13.8 us
    all_to_all x1, starting transfers between devices, per_device(): lax.all_to_all(halo_back.astype(jnp.bfloat16), 'dom', split_axis=0, conca...  10.3 us
    all_to_all x1, starting transfers between devices, per_device(): lax.all_to_all(hidden[None], 'snap', split_axis=1, concat_axis=0, tiled=T...  9.54 us
    reshape x2, local copies, waits for them, and re-layouts, struct_core(): keys_g = key_tab[links].reshape(row_count, slots, HEADS, head_dim)  8.84 us
  transfers between devices with their start and end apart: 6, of which 5 were waited for; matrix products, arithmetic and copies ran while one was open for 21% of the time, Pallas kernels for 0%

profile of v1, /device:TPU:1, one launch (start us, length us, event | category | flops | bytes accessed | tf_op | source)
XLA Modules:
  0.0 276.5 jit_solution(5463996496252345527)
XLA Ops:
  8.2 1.9 convolution_convert_fusion.1
  10.3 2.0 gather_fusion
  12.3 13.8 %all-to-all-start = ((bf16[32,8,1024]{2,1,0:T(8,128)(2,1)}), bf16[32,8,1024]{2,1,0:T(8,128)(2,1)S(1)}, u32[]{:S(2)}, u32[]{:S(2)}) async-start(bf16[32,8,1024]{2,1,0:T(8,128)(2,1)} %bitcast.7), calls=%async_computation | async-start | bytes 1048576 | tf_op jit(solution)/shard_map/all_to_all | solution.py:68
  27.8 14.6 %all-to-all-done = bf16[32,8,1024]{2,1,0:T(8,128)(2,1)S(1)} async-done(((bf16[32,8,1024]{2,1,0:T(8,128)(2,1)}), bf16[32,8,1024]{2,1,0:T(8,128)(2,1)S(1)}, u32[]{:S(2)}, u32[]{:S(2)}) %all-to-all-start) | async-done | bytes 524320 | tf_op jit(solution)/shard_map/all_to_all | solution.py:68
  44.3 5.1 %gather_fusion.1 = bf16[1024,512]{1,0:T(8,128)(2,1)} fusion(bf16[384,512]{1,0:T(8,128)(2,1)S(1)} %get-tuple-element.3, s32[1024]{0:T(1024)S(1)} %get-tuple-element.20), kind=kCustom, calls=%fused_computation.1 | custom fusion | bytes 2101248 | tf_op jit(solution)/shard_map/gather | solution.py:25
  49.3 4.0 %reshape.244 = bf16[128,8,8,64]{3,2,1,0:T(8,128)(2,1)} reshape(bf16[1024,512]{1,0:T(8,128)(2,1)} %gather_fusion.1) | data formatting | bytes 2097152 | tf_op jit(solution)/shard_map/reshape | solution.py:25
  53.3 3.6 %multiply_reduce_fusion.3 = f32[128,8,8]{1,2,0:T(8,128)} fusion(f32[128,8,64]{2,1,0:T(8,128)S(1)} %copy.120, bf16[128,8,8,64]{3,2,1,0:T(8,128)(2,1)} %reshape.244), kind=kLoop, calls=%fused_computation.10 | loop fusion | flops 1564672 | bytes 1343488
  59.4 5.1 %gather_fusion.2 = bf16[1024,512]{1,0:T(8,128)(2,1)} fusion(bf16[384,512]{1,0:T(8,128)(2,1)S(1)} %get-tuple-element.2, s32[1024]{0:T(1024)S(1)} %get-tuple-element.20), kind=kCustom, calls=%fused_computation.2 | custom fusion | bytes 2101248 | tf_op jit(solution)/shard_map/gather | solution.py:26
  64.5 4.0 %reshape.246 = bf16[128,8,8,64]{3,2,1,0:T(8,128)(2,1)} reshape(bf16[1024,512]{1,0:T(8,128)(2,1)} %gather_fusion.2) | data formatting | bytes 2097152 | tf_op jit(solution)/shard_map/reshape | solution.py:26
  68.5 2.6 multiply_reduce_fusion.2
  75.2 9.5 %all-to-all-start.1 = ((bf16[16,2,2048]{2,1,0:T(2,128)(2,1)}), bf16[16,2,2048]{2,1,0:T(2,128)(2,1)S(1)}, u32[]{:S(2)}, u32[]{:S(2)}) async-start(bf16[16,2,2048]{2,1,0:T(2,128)(2,1)} %reshape.338), calls=%async_computation.1 | async-start | bytes 262144 | tf_op jit(solution)/shard_map/all_to_all | solution.py:77
  85.3 8.3 %all-to-all-done.1 = bf16[16,2,2048]{2,1,0:T(2,128)(2,1)S(1)} async-done(((bf16[16,2,2048]{2,1,0:T(2,128)(2,1)}), bf16[16,2,2048]{2,1,0:T(2,128)(2,1)S(1)}, u32[]{:S(2)}, u32[]{:S(2)}) %all-to-all-start.1) | async-done | bytes 131104 | tf_op jit(solution)/shard_map/all_to_all | solution.py:77
  100.6 2.1 fusion.76
  103.6 2.3 fusion.10
  105.9 2.2 fusion.11
  116.4 2.8 %fusion.1 = bf16[512,1536]{1,0:T(8,128)(2,1)} fusion(bf16[16,8,1536]{2,1,0:T(8,128)(2,1)} %constant_dynamic-update-slice_fusion, f32[16,512]{1,0:T(8,128)S(1)} %convert_element_type.112, bf16[1,128,512]{2,0,1:T(2,128)(2,1)S(1)} %bitcast.134), kind=kOutput, calls=%fused_computation.14 | convolution fusion | flops 202309632 | bytes 2129920 | tf_op jit(solution)/shard_map/dot_general | solution.py:95
  119.3 51.0 %reduce-scatter.2.cloned.1.call-done = bf16[32,1536]{1,0:T(8,128)(2,1)} async-done(((bf16[512,1536]{1,0:T(8,128)(2,1)}), bf16[32,1536]{1,0:T(8,128)(2,1)}) %reduce-scatter.2.cloned.1.call-update) | async-done | bytes 98320 | tf_op jit(solution)/shard_map/reduce_scatter | solution.py:98
  171.7 6.8 %all-to-all-start.2 = ((bf16[16,8,512]{2,1,0:T(8,128)(2,1)}), bf16[16,8,512]{2,1,0:T(8,128)(2,1)S(1)}, u32[]{:S(2)}, u32[]{:S(2)}) async-start(bf16[16,8,512]{2,1,0:T(8,128)(2,1)} %fusion.17), calls=%async_computation.2 | async-start | bytes 262144 | tf_op jit(solution)/shard_map/all_to_all | solution.py:103
  179.4 7.9 %all-to-all-done.2 = bf16[16,8,512]{2,1,0:T(8,128)(2,1)S(1)} async-done(((bf16[16,8,512]{2,1,0:T(8,128)(2,1)}), bf16[16,8,512]{2,1,0:T(8,128)(2,1)S(1)}, u32[]{:S(2)}, u32[]{:S(2)}) %all-to-all-start.2) | async-done | bytes 131104 | tf_op jit(solution)/shard_map/all_to_all | solution.py:103
  188.0 5.6 %multiply_reduce_fusion.1 = (bf16[128,8,8]{1,2,0:T(8,128)(2,1)S(1)}, f32[128,8,8,64]{3,2,1,0:T(8,128)}) fusion(f32[128,8,64]{2,1,0:T(8,128)S(1)} %copy.122, bf16[128,8,8,64]{3,2,1,0:T(8,128)(2,1)} %reshape.246, f32[128,8,8]{1,2,0:T(8,128)} %copy.90), kind=kLoop, calls=%fused_computation.8 | loop fusion | flops 2088960 | bytes 3457024
  193.6 4.8 %reshape.300 = f32[1024,512]{1,0:T(8,128)} reshape(f32[128,8,8,64]{3,2,1,0:T(8,128)} %get-tuple-element.7) | data formatting | bytes 4194304 | tf_op jit(solution)/shard_map/transpose(jvp())/reshape | solution.py:26
  198.9 5.6 %multiply_reduce_fusion = (bf16[128,8,64]{2,1,0:T(8,128)(2,1)}, f32[128,8,8,64]{3,2,1,0:T(8,128)}) fusion(f32[128,8,8]{1,2,0:T(8,128)S(1)} %copy.123, bf16[128,8,8,64]{3,2,1,0:T(8,128)(2,1)} %reshape.244, f32[128,8,64]{2,1,0:T(8,128)S(1)} %copy.120), kind=kLoop, calls=%fused_computation.7 | loop fusion | flops 2031616 | bytes 3571712
  204.5 4.9 %reshape.292 = f32[1024,512]{1,0:T(8,128)} reshape(f32[128,8,8,64]{3,2,1,0:T(8,128)} %get-tuple-element.5) | data formatting | bytes 4194304 | tf_op jit(solution)/shard_map/transpose(jvp())/reshape | solution.py:25
  209.4 7.4 %scatter_custom_fusion.1 = f32[384,512]{1,0:T(8,128)S(1)} fusion(s32[1024]{0:T(1024)S(1)} %reshape.274, f32[1024,512]{1,0:T(8,128)} %reshape.300, f32[]{:T(128)} %constant.16.clone.1), kind=kCustom, calls=%fused_computation.65 | custom fusion | flops 524288 | bytes 786944 | tf_op jit(solution)/shard_map/transpose(jvp())/scatter-add | solution.py:26
  216.8 7.5 %scatter_custom_fusion = f32[384,512]{1,0:T(8,128)S(1)} fusion(s32[1024]{0:T(1024)S(1)} %reshape.274, f32[1024,512]{1,0:T(8,128)} %reshape.292, f32[]{:T(128)} %constant.16.clone.1), kind=kCustom, calls=%fused_computation.67 | custom fusion | flops 524288 | bytes 786944 | tf_op jit(solution)/shard_map/transpose(jvp())/scatter-add | solution.py:25
  225.4 10.3 %all-to-all-start.3 = ((bf16[32,8,1024]{2,1,0:T(8,128)(2,1)}), bf16[32,8,1024]{2,1,0:T(8,128)(2,1)}, u32[]{:S(2)}, u32[]{:S(2)}) async-start(bf16[32,8,1024]{2,1,0:T(8,128)(2,1)} %maximum_bitcast_fusion), calls=%async_computation.3 | async-start | bytes 1048576 | tf_op jit(solution)/shard_map/all_to_all | solution.py:118
  235.7 1.8 slice.61
  240.9 1.8 pad_maximum_fusion
  242.7 15.7 %all-to-all-done.3 = bf16[32,8,1024]{2,1,0:T(8,128)(2,1)} async-done(((bf16[32,8,1024]{2,1,0:T(8,128)(2,1)}), bf16[32,8,1024]{2,1,0:T(8,128)(2,1)}, u32[]{:S(2)}, u32[]{:S(2)}) %all-to-all-start.3) | async-done | bytes 524320 | tf_op jit(solution)/shard_map/all_to_all | solution.py:118
  258.4 5.0 %scatter_custom_fusion.2 = f32[128,1024]{1,0:T(8,128)} fusion(f32[128,1024]{1,0:T(8,128)} %pad_maximum_fusion, s32[256]{0:T(256)S(1)} %bitcast.141, bf16[32,8,1024]{2,1,0:T(8,128)(2,1)} %all-to-all-done.3), kind=kCustom, calls=%fused_computation.39 | custom fusion | flops 524288 | bytes 1048576 | tf_op jit(solution)/shard_map/scatter-add | solution.py:125
  264.4 2.2 fusion.20
  266.6 2.3 reduce_sum.64
  (117 shorter events, 37.6 us)
Async XLA Ops:
  7.2 86.6 %copy-start = (bf16[512,1536]{1,0:T(8,128)(2,1)S(1)}, bf16[512,1536]{1,0:T(8,128)(2,1)}, u32[]{:S(2)}) copy-start(bf16[512,1536]{1,0:T(8,128)(2,1)} %param.12) | copy-start | bytes 4718596
  7.2 2.9 %copy-start.15 = (s32[1,1,32,8]{2,3,1,0:T(8,128)S(1)}, s32[1,1,32,8]{2,3,1,0:T(8,128)}, u32[]{:S(2)}) copy-start(s32[1,1,32,8]{2,3,1,0:T(8,128)} %param.17) | copy-start | bytes 3076
  10.3 15.8 %copy-start.12 = (bf16[1,128,512]{2,1,0:T(8,128)(2,1)S(1)}, bf16[1,128,512]{2,1,0:T(8,128)(2,1)}, u32[]{:S(2)}) copy-start(bf16[1,128,512]{2,1,0:T(8,128)(2,1)} %param.10) | copy-start | bytes 393220
  12.3 15.0 %copy-start.17 = (s32[16,8]{0,1:T(8,128)S(1)}, s32[16,8]{0,1:T(8,128)}, u32[]{:S(2)}) copy-start(s32[16,8]{0,1:T(8,128)} %param.18) | copy-start | bytes 1540
  12.3 30.1 %all-to-all-start = ((bf16[32,8,1024]{2,1,0:T(8,128)(2,1)}), bf16[32,8,1024]{2,1,0:T(8,128)(2,1)S(1)}, u32[]{:S(2)}, u32[]{:S(2)}) async-start(bf16[32,8,1024]{2,1,0:T(8,128)(2,1)} %bitcast.7), calls=%async_computation | async-start | bytes 1048576 | tf_op jit(solution)/shard_map/all_to_all | solution.py:68
  42.4 0.8 copy-start.3
  53.3 4.8 %copy-start.16 = (s32[1,128,8]{1,2,0:T(8,128)S(1)}, s32[1,128,8]{1,2,0:T(8,128)}, u32[]{:S(2)}) copy-start(s32[1,128,8]{1,2,0:T(8,128)} %param.16) | copy-start | bytes 12292
  53.3 4.8 %copy-start.19 = (f32[4,8]{1,0:T(4,128)S(1)}, f32[4,8]{1,0:T(4,128)}, u32[]{:S(2)}) copy-start(f32[4,8]{1,0:T(4,128)} %param.14) | copy-start | bytes 388
  64.5 4.0 %copy-start.4 = (f32[128,8,8]{1,2,0:T(8,128)S(1)}, f32[128,8,8]{1,2,0:T(8,128)}, u32[]{:S(2)}) copy-start(f32[128,8,8]{1,2,0:T(8,128)} %copy.121) | copy-start | bytes 98308
  71.1 13.9 %copy-start.14 = (bf16[16,512]{1,0:T(8,128)(2,1)S(1)}, bf16[16,512]{1,0:T(8,128)(2,1)}, u32[]{:S(2)}) copy-start(bf16[16,512]{1,0:T(8,128)(2,1)} %param.13) | copy-start | bytes 49156
  71.1 13.9 %copy-start.10 = (bf16[16,8,512]{2,1,0:T(8,128)(2,1)S(1)}, bf16[16,8,512]{2,1,0:T(8,128)(2,1)}, u32[]{:S(2)}) copy-start(bf16[16,8,512]{2,1,0:T(8,128)(2,1)} %param.19) | copy-start | bytes 393220
  71.1 14.1 %copy-start.18 = (pred[16,8]{0,1:T(8,128)(4,1)S(1)}, pred[16,8]{0,1:T(8,128)(4,1)}, u32[]{:S(2)}) copy-start(pred[16,8]{0,1:T(8,128)(4,1)} %broadcast_compare_fusion) | copy-start | bytes 388
  75.2 18.4 %all-to-all-start.1 = ((bf16[16,2,2048]{2,1,0:T(2,128)(2,1)}), bf16[16,2,2048]{2,1,0:T(2,128)(2,1)S(1)}, u32[]{:S(2)}, u32[]{:S(2)}) async-start(bf16[16,2,2048]{2,1,0:T(2,128)(2,1)} %reshape.338), calls=%async_computation.1 | async-start | bytes 262144 | tf_op jit(solution)/shard_map/all_to_all | solution.py:77
  84.7 85.6 %reduce-scatter.2.cloned.1.call-start = ((), (), s32[]{:S(2)}) async-start(), calls=%async_computation.5 | async-start | bytes 1671168 | tf_op jit(solution)/shard_map/reduce_scatter | solution.py:98
  85.3 13.9 %copy-start.13 = (pred[16,16,8]{0,1,2:T(8,128)(4,1)}, pred[16,16,8]{0,1,2:T(8,128)(4,1)S(1)}, u32[]{:S(2)}) copy-start(pred[16,16,8]{0,1,2:T(8,128)(4,1)S(1)} %or_and_fusion) | copy-start | bytes 6148
  93.8 1.2 copy-start.8
  96.0 6.7 %copy-start.6 = (bf16[16,8,8,64]{3,2,1,0:T(8,128)(2,1)}, bf16[16,8,8,64]{3,2,1,0:T(8,128)(2,1)S(1)}, u32[]{:S(2)}) copy-start(bf16[16,8,8,64]{3,2,1,0:T(8,128)(2,1)S(1)} %reshape.251) | copy-start | bytes 393220
  99.2 3.5 %copy-start.5 = (bf16[16,16,8,8]{0,1,3,2:T(8,128)(2,1)S(1)}, bf16[16,16,8,8]{0,1,3,2:T(8,128)(2,1)}, u32[]{:S(2)}) copy-start(bf16[16,16,8,8]{0,1,3,2:T(8,128)(2,1)} %fusion.9) | copy-start | bytes 98308
  108.1 8.2 %copy-start.9 = (bf16[128,1,512]{2,1,0:T(2,128)(2,1)S(1)}, bf16[128,1,512]{2,1,0:T(2,128)(2,1)}, u32[]{:S(2)}) copy-start(bf16[128,1,512]{2,1,0:T(2,128)(2,1)} %copy-done.8) | copy-start | bytes 393220
  116.4 54.0 %copy-start.7 = (bf16[16,8,1536]{2,1,0:T(8,128)(2,1)S(1)}, bf16[16,8,1536]{2,1,0:T(8,128)(2,1)}, u32[]{:S(2)}) copy-start(bf16[16,8,1536]{2,1,0:T(8,128)(2,1)} %constant_dynamic-update-slice_fusion) | copy-start | bytes 1179652
  116.4 54.0 %copy-start.11 = (bf16[16,8,512]{2,1,0:T(8,128)(2,1)S(1)}, bf16[16,8,512]{2,1,0:T(8,128)(2,1)}, u32[]{:S(2)}) copy-start(bf16[16,8,512]{2,1,0:T(8,128)(2,1)} %param.19) | copy-start | bytes 393220
  119.2 147.4 %all-gather.3.cloned.1.call-start = ((), (), s32[]{:S(2)}) async-start(), calls=%async_computation.6 | async-start | bytes 3244032 | tf_op jit(solution)/shard_map/all_gather | solution.py:10
  171.7 15.7 %all-to-all-start.2 = ((bf16[16,8,512]{2,1,0:T(8,128)(2,1)}), bf16[16,8,512]{2,1,0:T(8,128)(2,1)S(1)}, u32[]{:S(2)}, u32[]{:S(2)}) async-start(bf16[16,8,512]{2,1,0:T(8,128)(2,1)} %fusion.17), calls=%async_computation.2 | async-start | bytes 262144 | tf_op jit(solution)/shard_map/all_to_all | solution.py:103
  224.3 11.4 %copy-start.2 = (f32[384,512]{1,0:T(8,128)}, f32[384,512]{1,0:T(8,128)S(1)}, u32[]{:S(2)}) copy-start(f32[384,512]{1,0:T(8,128)S(1)} %scatter_custom_fusion) | copy-start | bytes 2359300
  225.4 33.0 %all-to-all-start.3 = ((bf16[32,8,1024]{2,1,0:T(8,128)(2,1)}), bf16[32,8,1024]{2,1,0:T(8,128)(2,1)}, u32[]{:S(2)}, u32[]{:S(2)}) async-start(bf16[32,8,1024]{2,1,0:T(8,128)(2,1)} %maximum_bitcast_fusion), calls=%async_computation.3 | async-start | bytes 1048576 | tf_op jit(solution)/shard_map/all_to_all | solution.py:118
  235.7 28.7 %copy-start.1 = (bf16[512,1536]{1,0:T(8,128)(2,1)S(1)}, bf16[512,1536]{1,0:T(8,128)(2,1)}, u32[]{:S(2)}) copy-start(bf16[512,1536]{1,0:T(8,128)(2,1)} %param.11) | copy-start | bytes 4718596
Sparse Core Ops, SparseCore 0:
  119.4 50.9 reduce-scatter.1
  173.5 91.0 all-gather.2
